TPU v7x, 32 devices: a whole 2x2x4 slice. The times are simulated.
32 devices in a mesh: gene: 4 (over z), var: 4 (over y, core), perm: 2 (over x).
Axes of the slice: x: 2, y: 2, z: 4, core: 2. Of those that a mesh axis runs over, the one named last changes fastest.
Arguments:
- genotypes: bfloat16 [4, 6144, 768], P('gene', ('var', 'perm')), may hold values from 0 to 2
- phenotypes: float32 [512, 768], P('gene'), may hold values from -6 to 6
- perm_rows: int32 [256, 768], P(('var', 'perm')), may hold values from 0 to 767, each once within a row
- starts: int32 [512], P('gene'), may hold values from 0 to 2048, as said below
Outputs:
- maxima: float32 [256, 512], P(('var', 'perm'), 'gene')
- moments: float32 [2, 512], P(None, 'gene')
- pooled: float32 [2], replicated
Inputs may be any that keep to these rules, and one draw needn't show every extreme that they name: `perm_rows`: each row is a permutation of 0 to 767. Within each block of 128 genes the starts never fall; a gene's window of 4096 variants lies inside its block's 6144 variants.
All inputs are finite; a program needn't handle non-finite values.
Results may differ from a plain program's by a relative error of at most 0.0023.
Values may be sent and summed in bfloat16 or wider, within the bound.
A program may use at most 64 MiB of HBM per device.

v0:
```python
import functools

import jax
import jax.numpy as jnp
from jax import lax
from jax.experimental import pallas as pl
from jax.experimental.pallas import tpu as pltpu
from jax.sharding import PartitionSpec as P

WINDOW = 4096
MESH = pl.DeviceIdType.MESH
UNROLL = 8


def standard_rows(values):
    as_float = values.astype(jnp.float32)
    centred = as_float - jnp.mean(as_float, axis=1, keepdims=True)
    inv_norm = lax.rsqrt(jnp.sum(centred * centred, axis=1, keepdims=True) + 1.0)
    return (centred * inv_norm).astype(jnp.bfloat16)


def kernel(
    sizes, geno, pheno, perms, starts, packed,
    rows, table, base, best, mask, stats, sums,
    send, recv, pass_send, pass_recv, far_send, far_recv, far_pass_send, far_pass_recv,
    stat_send, stat_recv, sum_send, sum_recv,
):
    n_gene, n_var, n_perm = sizes
    n_block = n_var * n_perm
    chips = n_block // 2
    quarter = rows.shape[1]
    half = 2 * quarter
    samples = rows.shape[2]
    width, genes = perms.shape[0], packed.shape[1]
    tiles, tile_cols, _ = table.shape
    per_tile = tile_cols // genes
    square = n_var == 4 and n_perm == 2

    gene_at = lax.axis_index("gene")
    var_at = lax.axis_index("var")
    perm_at = lax.axis_index("perm")
    core = lax.rem(var_at, 2)
    chip = (var_at // 2) * n_perm + perm_at
    me = var_at * n_perm + perm_at

    def device_of(chip_at, core_at):
        return {"var": (chip_at // n_perm) * 2 + core_at, "perm": lax.rem(chip_at, n_perm)}

    def block_of(chip_at, core_at):
        return ((chip_at // n_perm) * 2 + core_at) * n_perm + lax.rem(chip_at, n_perm)

    def block_peer(step):
        other = lax.rem(me + step, n_block)
        return {"var": other // n_perm, "perm": lax.rem(other, n_perm)}

    def gene_peer(step):
        return {"gene": lax.rem(gene_at + step, n_gene)}

    barrier = pltpu.get_barrier_semaphore()
    for step in range(1, n_block):
        pl.semaphore_signal(barrier, inc=1, device_id=block_peer(step), device_id_type=MESH)
    for step in range(1, n_gene):
        pl.semaphore_signal(barrier, inc=1, device_id=gene_peer(step), device_id_type=MESH)

    for part in range(2):
        ready = standard_rows(geno[pl.ds(part * half, half), :])
        rows[me * 4 + part * 2] = ready[:quarter]
        rows[me * 4 + part * 2 + 1] = ready[quarter:]
    base[...] = standard_rows(pheno[...])
    best[...] = jnp.zeros_like(best)
    pl.semaphore_wait(barrier, n_block - 1 + n_gene - 1)

    def shift(step, back=False):
        if square:
            flip_y, flip_x = step // 2, step % 2
            y, x = chip // 2, lax.rem(chip, 2)
            y = 1 - y if flip_y else y
            x = 1 - x if flip_x else x
            return y * 2 + x
        return lax.rem(chip + (chips - step if back else step), chips)

    waiting = []

    def start(chunk, count, target, send_sem, recv_sem):
        piece = rows.at[pl.ds(chunk, count)]
        copy = pltpu.make_async_remote_copy(
            src_ref=piece, dst_ref=piece, send_sem=send_sem,
            recv_sem=recv_sem, device_id=target, device_id_type=MESH,
        )
        copy.start()
        waiting.append(copy)

    def arrive(chunk, count, recv_sem):
        piece = rows.at[pl.ds(chunk, count)]
        pltpu.make_async_remote_copy(
            src_ref=piece, dst_ref=piece, send_sem=send.at[0, 0],
            recv_sem=recv_sem, device_id=partner, device_id_type=MESH,
        ).wait_recv()

    partner = device_of(chip, 1 - core)

    def to_chip(step, part):
        start(
            me * 4 + part * 2, 2, device_of(shift(step), core),
            send.at[step, part], recv.at[step, part],
        )

    def to_partner(chunk, step, part):
        start(chunk, 2, partner, pass_send.at[step, part], pass_recv.at[step, part])

    if square:
        to_chip(1, 0)
        to_chip(2, 1)
        to_partner(me * 4, 0, 0)
        to_partner(me * 4 + 2, 0, 1)
        to_chip(1, 1)
        to_chip(2, 0)
    else:
        to_partner(me * 4, 0, 0)
        to_partner(me * 4 + 2, 0, 1)
        for step in range(1, chips):
            for part in range(2):
                to_chip(step, part)

    def build(at, carry):
        for pair in range(per_tile):
            order = perms[pl.ds(at * per_tile + pair, 1), :]
            picked = lax.broadcasted_iota(jnp.int32, (samples, samples), 0) == order
            select = jnp.where(picked, 1.0, 0.0).astype(jnp.bfloat16)
            placed = jnp.dot(base[...], select, preferred_element_type=jnp.float32)
            table[at, pl.ds(pair * genes, genes), :] = placed.astype(jnp.bfloat16)
        return carry

    lax.fori_loop(0, tiles, build, 0)

    unroll = min(UNROLL, tiles)

    def score(chunks):
        def one_chunk(at, carry):
            pieces = chunks[0]
            for place in range(1, len(chunks)):
                pieces = [jnp.where(at == place, new, old) for new, old in zip(chunks[place], pieces)]
            first = starts[...]
            for place, piece in enumerate(pieces):
                row = piece * quarter + lax.broadcasted_iota(jnp.int32, (quarter, genes), 0)
                inside = (row >= first) & (row < first + WINDOW)
                mask[pl.ds(place * quarter, quarter), :] = jnp.where(inside, 1.0, 0.0)

            def some_tiles(group, inner):
                for place in range(unroll):
                    tile = group * unroll + place
                    found = lax.dot_general(
                        jnp.concatenate([rows[piece] for piece in pieces], axis=0), table[tile], (((1,), (1,)), ((), ())),
                        preferred_element_type=jnp.float32,
                    )
                    for pair in range(per_tile):
                        part = found[:, pair * genes:(pair + 1) * genes]
                        part = part * part * mask[...]
                        top = jnp.max(part.reshape(half // 8, 8, genes), axis=0)
                        slot = tile * per_tile + pair
                        best[slot] = jnp.maximum(best[slot], top)
                return inner

            return lax.fori_loop(0, tiles // unroll, some_tiles, carry)

        lax.fori_loop(0, len(chunks), one_chunk, 0)

    def chunk_at(step, core_at, part):
        return block_of(shift(step, back=True) if step else chip, core_at) * 4 + part * 2

    def halves(arrivals, core_at):
        found = [chunk_at(step, core_at, part) for step, part in arrivals]
        return [(chunk, chunk + 1) for chunk in found]

    def stage(arrivals, relay):
        if arrivals[0][0]:
            for step, part in arrivals:
                chunk = chunk_at(step, core, part)
                arrive(chunk, 2, recv.at[step, part])
                if relay:
                    target = device_of(shift(3 - step), core)
                    for piece in range(2):
                        start(
                            chunk + piece, 1, target,
                            far_send.at[part, piece], far_recv.at[part, piece],
                        )
                to_partner(chunk, step, part)
        score(halves(arrivals, core))
        for step, part in arrivals:
            arrive(chunk_at(step, 1 - core, part), 2, pass_recv.at[step, part])
        score(halves(arrivals, 1 - core))

    def far_stage(piece):
        own = [chunk_at(3, core, part) + piece for part in range(2)]
        passed = [chunk_at(3, 1 - core, part) + piece for part in range(2)]
        for part in range(2):
            arrive(own[part], 1, far_recv.at[part, piece])
            start(
                own[part], 1, partner,
                far_pass_send.at[part, piece], far_pass_recv.at[part, piece],
            )
        score([own])
        for part in range(2):
            arrive(passed[part], 1, far_pass_recv.at[part, piece])
        score([passed])

    stage([(0, 0), (0, 1)], False)
    if square:
        stage([(1, 0), (2, 1)], True)
        stage([(1, 1), (2, 0)], False)
        far_stage(0)
        far_stage(1)
    else:
        for step in range(1, chips):
            stage([(step, 0), (step, 1)], False)

    top = jnp.max(best[...], axis=1) * samples
    packed[pl.ds(0, width), :] = top
    log_stat = jnp.log1p(top)
    total = jnp.sum(log_stat, axis=0, keepdims=True)
    total_sq = jnp.sum(log_stat * log_stat, axis=0, keepdims=True)
    line = lax.broadcasted_iota(jnp.int32, (8, genes), 0)
    stats[me] = jnp.where(line == 0, total, jnp.where(line == 1, total_sq, 0.0))
    exchange = []
    for step in range(1, n_block):
        copy = pltpu.make_async_remote_copy(
            src_ref=stats.at[me], dst_ref=stats.at[me], send_sem=stat_send.at[step],
            recv_sem=stat_recv.at[step], device_id=block_peer(step), device_id_type=MESH,
        )
        copy.start()
        exchange.append(copy)
    for step, copy in enumerate(exchange, 1):
        other = lax.rem(me + n_block - step, n_block)
        pltpu.make_async_remote_copy(
            src_ref=stats.at[other], dst_ref=stats.at[other], send_sem=stat_send.at[step],
            recv_sem=stat_recv.at[step], device_id=partner, device_id_type=MESH,
        ).wait_recv()
    mean = jnp.sum(stats[...], axis=0) / (width * n_block)
    sums[gene_at] = mean
    for step in range(1, n_gene):
        copy = pltpu.make_async_remote_copy(
            src_ref=sums.at[gene_at], dst_ref=sums.at[gene_at], send_sem=sum_send.at[step],
            recv_sem=sum_recv.at[step], device_id=gene_peer(step), device_id_type=MESH,
        )
        copy.start()
        exchange.append(copy)
    for step in range(1, n_gene):
        other = lax.rem(gene_at + n_gene - step, n_gene)
        pltpu.make_async_remote_copy(
            src_ref=sums.at[other], dst_ref=sums.at[other], send_sem=sum_send.at[step],
            recv_sem=sum_recv.at[step], device_id=partner, device_id_type=MESH,
        ).wait_recv()
    whole = jnp.sum(sums[...], axis=0)
    overall = jnp.sum(whole, axis=1, keepdims=True) / (genes * n_gene)
    spread = pltpu.roll(jnp.broadcast_to(overall, (8, genes)), 2, 0)
    packed[pl.ds(width, 8), :] = jnp.where(line < 2, mean, spread)
    for copy in waiting + exchange:
        copy.wait_send()


def unpack(packed, maxima, moments, pooled):
    width = maxima.shape[0]
    maxima[...] = packed[pl.ds(0, width), :]
    moments[...] = packed[pl.ds(width, 2), :]
    for place in range(2):
        pooled[place] = packed[width + 2 + place, 0]


def solution(mesh):
    n_gene, n_var, n_perm = (mesh.shape[name] for name in ("gene", "var", "perm"))
    n_block = n_var * n_perm

    def shards(genotypes, phenotypes, perm_rows, starts):
        _, local_rows, samples = genotypes.shape
        genes = phenotypes.shape[0]
        width = perm_rows.shape[0]
        quarter = local_rows // 4
        per_tile = max(256 // genes, 1)
        tiles = width // per_tile
        chips = n_block // 2
        steps = max(chips, 4)
        dma = pltpu.SemaphoreType.DMA
        vmem = pl.BlockSpec(memory_space=pltpu.VMEM)
        flops = 2 * width * genes * samples * (local_rows * n_block + samples)
        packed = pl.pallas_call(
            functools.partial(kernel, (n_gene, n_var, n_perm)),
            out_shape=jax.ShapeDtypeStruct((width + 8, genes), jnp.float32),
            in_specs=[vmem] * 4,
            out_specs=vmem,
            scratch_shapes=[
                pltpu.VMEM((n_block * 4, quarter, samples), jnp.bfloat16),
                pltpu.VMEM((tiles, per_tile * genes, samples), jnp.bfloat16),
                pltpu.VMEM((genes, samples), jnp.bfloat16),
                pltpu.VMEM((width, 8, genes), jnp.float32),
                pltpu.VMEM((2 * quarter, genes), jnp.float32),
                pltpu.VMEM((n_block, 8, genes), jnp.float32),
                pltpu.VMEM((n_gene, 8, genes), jnp.float32),
                dma((steps, 2)), dma((steps, 2)), dma((steps, 2)), dma((steps, 2)),
                dma((2, 2)), dma((2, 2)), dma((2, 2)), dma((2, 2)),
                dma((n_block,)), dma((n_block,)), dma((n_gene,)), dma((n_gene,)),
            ],
            compiler_params=pltpu.CompilerParams(
                collective_id=0, has_side_effects=True, vmem_limit_bytes=56 * 1024 * 1024
            ),
            cost_estimate=pl.CostEstimate(
                flops=flops, bytes_accessed=local_rows * samples * 2, transcendentals=0
            ),
        )(genotypes[0], phenotypes, perm_rows, starts.reshape(1, genes))
        return pl.pallas_call(
            unpack,
            out_shape=(
                jax.ShapeDtypeStruct((width, genes), jnp.float32),
                jax.ShapeDtypeStruct((2, genes), jnp.float32),
                jax.ShapeDtypeStruct((2,), jnp.float32),
            ),
            in_specs=[vmem],
            out_specs=(vmem, vmem, pl.BlockSpec(memory_space=pltpu.SMEM)),
        )(packed)

    return jax.shard_map(
        shards,
        mesh=mesh,
        in_specs=(
            P("gene", ("var", "perm"), None),
            P("gene", None),
            P(("var", "perm"), None),
            P("gene"),
        ),
        out_specs=(P(("var", "perm"), "gene"), P(None, "gene"), P()),
        check_vma=False,
    )
```

profile of v0, /device:TPU:0, one launch (start us, length us, event | category | flops | bytes accessed | tf_op | source)
XLA Modules:
  0.0 70.5 jit_solution(11353110833288217997)
XLA Ops:
  0.6 68.5 %shard_map.67.packed = f32[40,128]{1,0:T(8,128)} custom-call(bf16[768,768]{1,0:T(8,128)(2,1)} %bitcast.2, f32[128,768]{1,0:T(8,128)} %pheno.1, s32[32,768]{1,0:T(8,128)} %perms.1, s32[1,128]{1,0:T(1,128)} %bitcast.3), custom_call_target="tpu_custom_call" | custom-call | flops 43486543872 | bytes 1179648 | tf_op jit(solution)/shard_map/pallas_call | solution.py:285
  69.1 1.3 %shard_map.68 = (f32[32,128]{1,0:T(8,128)}, f32[2,128]{1,0:T(2,128)}, f32[2]{0:T(128)}) custom-call(f32[40,128]{1,0:T(8,128)} %shard_map.67.packed), custom_call_target="tpu_custom_call" | custom-call | tf_op jit(solution)/shard_map/pallas_call | solution.py:309
where the time goes:
time: 70.7 us; the launch traced here: 70.5 us
  Pallas kernels  69.8 us (99%)
    pallas_call x1, Pallas kernels, shards(): pl.pallas_call(functools.partial(kernel, (n_gene, n_var, n_perm)), out_sh...  68.5 us

commit v1 on v0

v1 whole, which is shorter than its diff:
```python
import functools

import jax
import jax.numpy as jnp
from jax import lax
from jax.experimental import pallas as pl
from jax.experimental.pallas import tpu as pltpu
from jax.sharding import PartitionSpec as P

WINDOW = 4096
MESH = pl.DeviceIdType.MESH
GROUP = 8
PAD = 16


def standard_rows(values):
    as_float = values.astype(jnp.float32)
    centred = as_float - jnp.mean(as_float, axis=1, keepdims=True)
    inv_norm = lax.rsqrt(jnp.sum(centred * centred, axis=1, keepdims=True) + 1.0)
    return (centred * inv_norm).astype(jnp.bfloat16)


def kernel(
    sizes, geno, pheno, perms, starts, firsts, packed,
    rows, table, base, lane_starts, best, partial, inbox, others, stats,
    own_send, own_recv, far_send, far_recv, pass_send, pass_recv,
    perm_send, perm_recv, top_send, top_recv, stat_send, stat_recv,
):
    n_gene, n_var, n_perm = sizes
    n_block = n_var * n_perm
    n_all = n_block * n_gene
    chips = n_var // 2
    local, samples = geno.shape
    strips = local // PAD
    width, genes = perms.shape[0], pheno.shape[0]
    groups = genes // GROUP
    cols = width * GROUP
    lanes = lane_starts.shape[2]
    span = local * n_block
    slack = 3 * span // 4 - WINDOW
    windowed = n_var == 4 and slack >= 0 and WINDOW >= span // 2
    fat = (span - WINDOW) // (slack + 1) if windowed else 0

    gene_at = lax.axis_index("gene")
    var_at = lax.axis_index("var")
    perm_at = lax.axis_index("perm")
    core = lax.rem(var_at, 2)
    chip = var_at // 2
    here = (gene_at * n_var + var_at) * n_perm + perm_at

    def device_at(place):
        in_block = lax.rem(place, n_block)
        return {"gene": place // n_block, "var": in_block // n_perm, "perm": lax.rem(in_block, n_perm)}

    def var_of(step, core_of):
        return lax.rem(chip + step, chips) * 2 + core_of

    def place_of(var):
        if not windowed:
            return var * strips
        outer = jnp.where(var == 3, strips, 0)
        return jnp.where((var == 1) | (var == 2), 1 + (var + 1) * strips, outer)

    def first_row(var):
        return (var * n_perm + perm_at) * local

    def block(var, part=None):
        at = place_of(var)
        if part is None:
            return rows.at[pl.ds(at, strips)]
        return rows.at[pl.ds(at + part * (strips // 2), strips // 2)]

    partner = {"var": var_of(0, 1 - core)}

    barrier = pltpu.get_barrier_semaphore()
    for step in range(1, n_all):
        pl.semaphore_signal(
            barrier, inc=1, device_id=device_at(lax.rem(here + step, n_all)), device_id_type=MESH
        )

    base[...] = standard_rows(pheno[...])
    if windowed:
        rows[2 * strips] = jnp.zeros((PAD, samples), jnp.bfloat16)
    mine = block(var_at)
    for part in range(4):
        ready = standard_rows(geno[pl.ds(part * (local // 4), local // 4), :])
        mine[pl.ds(part * (strips // 4), strips // 4)] = ready.reshape(strips // 4, PAD, samples)
    best[...] = jnp.zeros_like(best)
    lane = lax.broadcasted_iota(jnp.int32, (groups, lanes), 1)
    group_line = lax.broadcasted_iota(jnp.int32, (groups, lanes), 0)
    own_lane = lane // GROUP == group_line
    spread = jnp.where(own_lane, jnp.broadcast_to(starts[...].astype(jnp.float32), (groups, lanes)), 0.0)
    shift = GROUP
    while shift < lanes:
        spread = spread + pltpu.roll(spread, shift, 1)
        shift *= 2
    lane_starts[...] = spread.astype(jnp.int32).reshape(groups, 1, lanes)

    def build(source, slot, begin, end):
        def pairs(at, carry):
            for inner in range(2):
                pair = at * 2 + inner
                placed = []
                for which in range(2):
                    order = source(pair * 2 + which).astype(jnp.int16)
                    picked = lax.broadcasted_iota(jnp.int16, (samples, samples), 0) == order
                    select = jnp.where(picked, jnp.bfloat16(1), jnp.bfloat16(0))
                    found = jnp.dot(base[...], select, preferred_element_type=jnp.float32)
                    placed.append(found.reshape(groups, GROUP, samples))
                both = jnp.concatenate(placed, axis=1).astype(jnp.bfloat16)
                table[slot, :, pl.ds(pl.multiple_of(pair * 2 * GROUP, 2 * GROUP), 2 * GROUP), :] = both
            return carry

        lax.fori_loop(begin, end, pairs, 0)

    turns = width // 4
    early = turns * 3 // 4
    build(lambda at: perms[pl.ds(at, 1), :], 0, 0, early)
    pl.semaphore_wait(barrier, n_all - 1)

    waiting = []

    def send(source, target, send_sem, recv_sem, dest=None):
        copy = pltpu.make_async_remote_copy(
            src_ref=source, dst_ref=source if dest is None else dest, send_sem=send_sem,
            recv_sem=recv_sem, device_id=target, device_id_type=MESH,
        )
        copy.start()
        return copy

    def receive(dest, recv_sem):
        pltpu.make_async_remote_copy(
            src_ref=dest, dst_ref=dest, send_sem=own_send.at[0], recv_sem=recv_sem,
            device_id=partner, device_id_type=MESH,
        ).wait_recv()

    def to_chips():
        for step in range(1, chips):
            for part in range(2):
                send(
                    block(var_at, part), {"var": var_of(step, core)},
                    far_send.at[step, part], far_recv.at[step, part],
                )

    is_mid = (var_at == 1) | (var_at == 2)
    for step in range(1, n_perm):
        waiting.append(send(
            perms, {"perm": lax.rem(perm_at + step, n_perm)},
            perm_send.at[step], perm_recv.at[step], others.at[step],
        ))
    waiting.append(send(block(var_at), partner, own_send.at[0], own_recv.at[0]))
    if windowed:
        pl.when(is_mid)(to_chips)
    else:
        to_chips()

    build(lambda at: perms[pl.ds(at, 1), :], 0, early, turns)

    def relay(step, part):
        piece = block(var_of(chips - step, core), part)
        receive(piece, far_recv.at[step, part])
        send(piece, partner, pass_send.at[step, part], pass_recv.at[step, part])

    def passed(step):
        for part in range(2):
            receive(block(var_of(chips - step, 1 - core), part), pass_recv.at[step, part])

    def relay_if(condition, part):
        pl.when(condition)(lambda: relay(1, part))

    for step in range(1, n_perm):
        receive(others.at[step], perm_recv.at[step])
        build(lambda at: others[step, pl.ds(at, 1), :], step, 0, turns)

    def top_of(values, slot, group, row):
        found = lax.dot_general(
            values, table[slot, group], (((1,), (1,)), ((), ())), preferred_element_type=jnp.float32
        )
        first = lane_starts[group]
        inside = (row >= first) & (row < first + WINDOW)
        height = values.shape[0]
        tops = []
        for piece in range(cols // lanes):
            part = found[:, piece * lanes:(piece + 1) * lanes]
            part = jnp.where(inside, part * part, 0.0)
            tops.append(jnp.max(part.reshape(height // 8, 8, lanes), axis=0))
        return jnp.concatenate(tops, axis=1)

    unroll = 4

    def score(var, begin=0, end=groups // unroll, slots=range(n_perm), unroll=unroll):
        row = first_row(var) + lax.broadcasted_iota(jnp.int32, (local, lanes), 0)
        values = block(var)

        def some(at, carry):
            for inner in range(unroll):
                group = at * unroll + inner
                for slot in slots:
                    top = top_of(values[...].reshape(local, samples), slot, group, row)
                    best[slot, group] = jnp.maximum(best[slot, group], top)
            return carry

        lax.fori_loop(begin, end, some, 0)

    def hand_over():
        for step in range(1, n_perm):
            partial[step] = jnp.max(best[step], axis=1) * samples
            waiting.append(send(
                partial.at[step], {"perm": lax.rem(perm_at + n_perm - step, n_perm)},
                top_send.at[step], top_recv.at[step], inbox.at[step],
            ))

    def strip_of(row, most):
        return lax.div(lax.min(lax.max(row, 0), most * PAD), PAD)

    def strips_at(begin, count):
        return jnp.concatenate([rows[begin + at] for at in range(count)], axis=0)

    def slide(slot):
        low = first_row(0)
        jump = first_row(3) - low - local
        height = local + PAD
        line = lax.broadcasted_iota(jnp.int32, (height, lanes), 0)

        def some(at, carry):
            for inner in range(2 * unroll):
                group = at * 2 * unroll + inner
                skip = strip_of(firsts[group * GROUP] - low, strips)
                spot = skip * PAD + line
                row = spot + low + jnp.where(spot >= local, jump, 0)
                values = strips_at(skip, strips + 1)
                top = top_of(values, slot, group, row)
                best[slot, group] = jnp.maximum(best[slot, group], top)
            return carry

        lax.fori_loop(0, groups // (2 * unroll), some, 0)

    def widen(slot):
        extent = [firsts[(group + 1) * GROUP - 1] - firsts[group * GROUP] for group in range(groups)]
        taken = [jnp.bool_(False)] * groups
        low, high = first_row(0), first_row(3)
        for place in range(fat):
            chosen, most, begin = jnp.int32(0), jnp.int32(-1), jnp.int32(0)
            for group in range(groups):
                better = jnp.logical_not(taken[group]) & (extent[group] > most)
                chosen = jnp.where(better, group, chosen)
                most = jnp.where(better, extent[group], most)
                begin = jnp.where(better, firsts[group * GROUP], begin)
            taken = [taken[group] | (chosen == group) for group in range(groups)]
            reach = (span - WINDOW) // (place + 1) - slack
            count = min(strips, (reach + 2 * PAD - 1) // PAD)
            skip = strip_of(begin - low, strips - count)
            row = high + skip * PAD + lax.broadcasted_iota(jnp.int32, (count * PAD, lanes), 0)
            values = strips_at(strips + skip, count)
            top = top_of(values, slot, chosen, row)
            for group in range(groups):
                added = jnp.where(chosen == group, top, 0.0)
                best[slot, group] = jnp.maximum(best[slot, group], added)

    if windowed:
        near_mid, near_outer = var_of(0, 1 - chip), var_of(0, chip)
        far_mid = var_of(1, chip)
        turn = groups // unroll
        is_outer = jnp.logical_not(is_mid)
        relay_if(is_outer, 0)
        pl.when(var_at != near_mid)(lambda: receive(block(near_mid), own_recv.at[0]))
        score(near_mid, 0, turn // 2)
        pl.when(is_outer)(to_chips)
        score(near_mid, turn // 2, turn * 3 // 4)
        relay_if(is_outer, 1)
        score(near_mid, turn * 3 // 4, turn)
        pl.when(is_mid)(lambda: passed(1))
        score(far_mid, 0, turn // 2)
        relay_if(is_mid, 0)
        score(far_mid, turn // 2, turn * 3 // 4)
        score(far_mid, turn * 3 // 2, turn * 2 - 1, unroll=unroll // 2)
        relay_if(is_mid, 1)
        score(far_mid, turn * 2 - 1, turn * 2, unroll=unroll // 2)
        pl.when(var_at != near_outer)(lambda: receive(block(near_outer), own_recv.at[0]))
        pl.when(is_outer)(lambda: passed(1))
        for slot in range(1, n_perm):
            slide(slot)
            widen(slot)
        hand_over()
        slide(0)
        widen(0)
    else:
        score(var_at)
        receive(block(var_of(0, 1 - core)), own_recv.at[0])
        score(var_of(0, 1 - core))
        for step in range(1, chips):
            for part in range(2):
                relay(step, part)
            score(var_of(chips - step, core))
            passed(step)
            score(var_of(chips - step, 1 - core))
        hand_over()

    partial[0] = jnp.max(best[0], axis=1) * samples
    for step in range(1, n_perm):
        receive(inbox.at[step], top_recv.at[step])
    top = partial[0]
    for step in range(1, n_perm):
        top = jnp.maximum(top, inbox[step])

    def over_perms(values):
        total = values[:, :lanes]
        for piece in range(1, cols // lanes):
            total = total + values[:, piece * lanes:(piece + 1) * lanes]
        shift = GROUP
        while shift < lanes:
            total = total + pltpu.roll(total, shift, 1)
            shift *= 2
        return jnp.sum(jnp.where(own_lane, total, 0.0), axis=0, keepdims=True)

    log_stat = jnp.log1p(top)
    stats[here, 0:1] = over_perms(log_stat)
    stats[here, 1:2] = over_perms(log_stat * log_stat)
    for step in range(1, n_all):
        waiting.append(send(
            stats.at[here], device_at(lax.rem(here + step, n_all)), stat_send.at[step], stat_recv.at[step],
        ))

    spot = lax.broadcasted_iota(jnp.int32, (cols, genes), 0)
    gene = lax.broadcasted_iota(jnp.int32, (cols, genes), 1)
    expand = jnp.where(own_lane, 1.0, 0.0)
    wide = lax.dot_general(
        top, expand, (((0,), (0,)), ((), ())), precision=lax.Precision.HIGHEST,
        preferred_element_type=jnp.float32,
    )
    wide = jnp.where(lax.rem(spot, GROUP) == lax.rem(gene, GROUP), wide, 0.0)
    packed[pl.ds(0, width), :] = jnp.sum(wide.reshape(width, GROUP, genes), axis=1)

    for step in range(1, n_all):
        receive(stats.at[lax.rem(here + n_all - step, n_all)], stat_recv.at[step])
    mean = jnp.sum(stats[pl.ds(gene_at * n_block, n_block)], axis=0) / (width * n_block)
    whole = jnp.sum(stats[...], axis=0) / (width * n_block)
    overall = jnp.sum(whole, axis=1, keepdims=True) / (genes * n_gene)
    packed[pl.ds(width, 2), :] = mean
    packed[pl.ds(width + 2, 2), :] = jnp.broadcast_to(overall, (2, genes))

    for step in range(1, chips):
        for part in range(2):
            pltpu.make_async_remote_copy(
                src_ref=block(var_at, part), dst_ref=block(var_at, part), send_sem=far_send.at[step, part],
                recv_sem=far_recv.at[step, part], device_id=partner, device_id_type=MESH,
            ).wait_send()
            pltpu.make_async_remote_copy(
                src_ref=block(var_at, part), dst_ref=block(var_at, part), send_sem=pass_send.at[step, part],
                recv_sem=pass_recv.at[step, part], device_id=partner, device_id_type=MESH,
            ).wait_send()
    for copy in waiting:
        copy.wait_send()


def unpack(packed, maxima, moments, pooled):
    width = maxima.shape[0]
    maxima[...] = packed[pl.ds(0, width), :]
    moments[...] = packed[pl.ds(width, 2), :]
    for place in range(2):
        pooled[place] = packed[width + 2 + place, 0]


def solution(mesh):
    n_gene, n_var, n_perm = (mesh.shape[name] for name in ("gene", "var", "perm"))
    n_block = n_var * n_perm
    n_all = n_block * n_gene

    def shards(genotypes, phenotypes, perm_rows, starts):
        _, local, samples = genotypes.shape
        genes = phenotypes.shape[0]
        width = perm_rows.shape[0]
        groups = genes // GROUP
        cols = width * GROUP
        chips = n_var // 2
        dma = pltpu.SemaphoreType.DMA
        vmem = pl.BlockSpec(memory_space=pltpu.VMEM)
        smem = pl.BlockSpec(memory_space=pltpu.SMEM)
        flops = 2 * width * genes * samples * (local * n_block + samples)
        packed = pl.pallas_call(
            functools.partial(kernel, (n_gene, n_var, n_perm)),
            out_shape=jax.ShapeDtypeStruct((width + 8, genes), jnp.float32),
            in_specs=[vmem] * 4 + [smem],
            out_specs=vmem,
            scratch_shapes=[
                pltpu.VMEM((n_var * local // PAD + 1, PAD, samples), jnp.bfloat16),
                pltpu.VMEM((n_perm, groups, cols, samples), jnp.bfloat16),
                pltpu.VMEM((genes, samples), jnp.bfloat16),
                pltpu.VMEM((groups, 1, genes), jnp.int32),
                pltpu.VMEM((n_perm, groups, 8, cols), jnp.float32),
                pltpu.VMEM((n_perm, groups, cols), jnp.float32),
                pltpu.VMEM((n_perm, groups, cols), jnp.float32),
                pltpu.VMEM((n_perm, width, samples), jnp.int32),
                pltpu.VMEM((n_all, 2, genes), jnp.float32),
                dma((1,)), dma((1,)), dma((chips, 2)), dma((chips, 2)), dma((chips, 2)), dma((chips, 2)),
                dma((n_perm,)), dma((n_perm,)), dma((n_perm,)), dma((n_perm,)),
                dma((n_all,)), dma((n_all,)),
            ],
            compiler_params=pltpu.CompilerParams(
                collective_id=0, has_side_effects=True, vmem_limit_bytes=56 * 1024 * 1024
            ),
            cost_estimate=pl.CostEstimate(
                flops=flops, bytes_accessed=local * samples * 2, transcendentals=0
            ),
        )(genotypes[0], phenotypes, perm_rows, starts.reshape(1, genes), starts)
        return pl.pallas_call(
            unpack,
            out_shape=(
                jax.ShapeDtypeStruct((width, genes), jnp.float32),
                jax.ShapeDtypeStruct((2, genes), jnp.float32),
                jax.ShapeDtypeStruct((2,), jnp.float32),
            ),
            in_specs=[vmem],
            out_specs=(vmem, vmem, pl.BlockSpec(memory_space=pltpu.SMEM)),
        )(packed)

    return jax.shard_map(
        shards,
        mesh=mesh,
        in_specs=(
            P("gene", ("var", "perm"), None),
            P("gene", None),
            P(("var", "perm"), None),
            P("gene"),
        ),
        out_specs=(P(("var", "perm"), "gene"), P(None, "gene"), P()),
        check_vma=False,
    )
```

time: 70.7 us -> 65.7 us (0.929)
  Pallas kernels: 69.8 us -> 64.7 us
    pallas_call x1, Pallas kernels: 68.5 us -> 63.3 us  [shards(): pl.pallas_call(functools.partial(kernel, (n_gene, n_var, n_perm)), out_sh...]
where the time goes in v1:
time: 65.7 us; the launch traced here: 65.5 us
  Pallas kernels  64.7 us (98%)
  between operations  0.8 us (1%)
    pallas_call x1, Pallas kernels, shards(): pl.pallas_call(functools.partial(kernel, (n_gene, n_var, n_perm)), out_sh...  63.3 us
    pallas_call x1, Pallas kernels, shards(): pl.pallas_call(unpack, out_shape=(jax.ShapeDtypeStruct((width, genes), jn...  1.35 us

profile of v1, /device:TPU:0, one launch (start us, length us, event | category | flops | bytes accessed | tf_op | source)
XLA Modules:
  0.0 65.5 jit_solution(13201103091388982119)
XLA Ops:
  0.6 63.3 %shard_map.67.packed = f32[40,128]{1,0:T(8,128)} custom-call(bf16[768,768]{1,0:T(8,128)(2,1)} %bitcast.2, f32[128,768]{1,0:T(8,128)} %pheno.1, s32[32,768]{1,0:T(8,128)} %perms.1, s32[1,128]{1,0:T(1,128)} %bitcast.3, s32[128]{0:T(128)} %firsts.1), custom_call_target="tpu_custom_call" | custom-call | flops 43486543872 | bytes 1179648 | tf_op jit(solution)/shard_map/pallas_call | solution.py:380
  64.0 1.3 %shard_map.68 = (f32[32,128]{1,0:T(8,128)}, f32[2,128]{1,0:T(2,128)}, f32[2]{0:T(128)}) custom-call(f32[40,128]{1,0:T(8,128)} %shard_map.67.packed), custom_call_target="tpu_custom_call" | custom-call | tf_op jit(solution)/shard_map/pallas_call | solution.py:406

commit v2 on v1

--- a/solution.py
+++ b/solution.py
@@ -22,7 +22,7 @@
 
 def kernel(
     sizes, geno, pheno, perms, starts, firsts, packed,
-    rows, table, base, lane_starts, best, partial, inbox, others, stats,
+    raw, raw_sem, rows, table, base, lane_starts, best, partial, inbox, others, stats,
     own_send, own_recv, far_send, far_recv, pass_send, pass_recv,
     perm_send, perm_recv, top_send, top_recv, stat_send, stat_recv,
 ):
@@ -72,6 +72,8 @@
 
     partner = {"var": var_of(0, 1 - core)}
 
+    fetch = pltpu.make_async_copy(geno, raw, raw_sem)
+    fetch.start()
     barrier = pltpu.get_barrier_semaphore()
     for step in range(1, n_all):
         pl.semaphore_signal(
@@ -79,12 +81,6 @@
         )
 
     base[...] = standard_rows(pheno[...])
-    if windowed:
-        rows[2 * strips] = jnp.zeros((PAD, samples), jnp.bfloat16)
-    mine = block(var_at)
-    for part in range(4):
-        ready = standard_rows(geno[pl.ds(part * (local // 4), local // 4), :])
-        mine[pl.ds(part * (strips // 4), strips // 4)] = ready.reshape(strips // 4, PAD, samples)
     best[...] = jnp.zeros_like(best)
     lane = lax.broadcasted_iota(jnp.int32, (groups, lanes), 1)
     group_line = lax.broadcasted_iota(jnp.int32, (groups, lanes), 0)
@@ -114,8 +110,15 @@
         lax.fori_loop(begin, end, pairs, 0)
 
     turns = width // 4
-    early = turns * 3 // 4
+    early = turns // 2
     build(lambda at: perms[pl.ds(at, 1), :], 0, 0, early)
+    if windowed:
+        rows[2 * strips] = jnp.zeros((PAD, samples), jnp.bfloat16)
+    mine = block(var_at)
+    fetch.wait()
+    for part in range(4):
+        ready = standard_rows(raw[pl.ds(part * (local // 4), local // 4), :])
+        mine[pl.ds(part * (strips // 4), strips // 4)] = ready.reshape(strips // 4, PAD, samples)
     pl.semaphore_wait(barrier, n_all - 1)
 
     waiting = []
@@ -168,9 +171,10 @@
     def relay_if(condition, part):
         pl.when(condition)(lambda: relay(1, part))
 
-    for step in range(1, n_perm):
-        receive(others.at[step], perm_recv.at[step])
-        build(lambda at: others[step, pl.ds(at, 1), :], step, 0, turns)
+    def build_others():
+        for step in range(1, n_perm):
+            receive(others.at[step], perm_recv.at[step])
+            build(lambda at: others[step, pl.ds(at, 1), :], step, 0, turns)
 
     def top_of(values, slot, group, row):
         found = lax.dot_general(
@@ -235,10 +239,10 @@
 
         lax.fori_loop(0, groups // (2 * unroll), some, 0)
 
-    def widen(slot):
+    def widest():
         extent = [firsts[(group + 1) * GROUP - 1] - firsts[group * GROUP] for group in range(groups)]
         taken = [jnp.bool_(False)] * groups
-        low, high = first_row(0), first_row(3)
+        found = []
         for place in range(fat):
             chosen, most, begin = jnp.int32(0), jnp.int32(-1), jnp.int32(0)
             for group in range(groups):
@@ -247,28 +251,37 @@
                 most = jnp.where(better, extent[group], most)
                 begin = jnp.where(better, firsts[group * GROUP], begin)
             taken = [taken[group] | (chosen == group) for group in range(groups)]
+            found.append((chosen, begin))
+        return found
+
+    def widen(slot, found):
+        low, high = first_row(0), first_row(3)
+        tops = []
+        for place, (chosen, begin) in enumerate(found):
             reach = (span - WINDOW) // (place + 1) - slack
             count = min(strips, (reach + 2 * PAD - 1) // PAD)
             skip = strip_of(begin - low, strips - count)
             row = high + skip * PAD + lax.broadcasted_iota(jnp.int32, (count * PAD, lanes), 0)
-            values = strips_at(strips + skip, count)
-            top = top_of(values, slot, chosen, row)
-            for group in range(groups):
-                added = jnp.where(chosen == group, top, 0.0)
-                best[slot, group] = jnp.maximum(best[slot, group], added)
+            tops.append(top_of(strips_at(strips + skip, count), slot, chosen, row))
+        for group in range(groups):
+            added = best[slot, group]
+            for (chosen, _), top in zip(found, tops):
+                added = jnp.maximum(added, jnp.where(chosen == group, top, 0.0))
+            best[slot, group] = added
 
     if windowed:
         near_mid, near_outer = var_of(0, 1 - chip), var_of(0, chip)
         far_mid = var_of(1, chip)
         turn = groups // unroll
         is_outer = jnp.logical_not(is_mid)
+        pl.when(var_at != near_mid)(lambda: receive(block(near_mid), own_recv.at[0]))
+        score(near_mid, 0, turn // 2, range(1), 2 * unroll)
+        build_others()
+        pl.when(is_outer)(to_chips)
         relay_if(is_outer, 0)
-        pl.when(var_at != near_mid)(lambda: receive(block(near_mid), own_recv.at[0]))
-        score(near_mid, 0, turn // 2)
-        pl.when(is_outer)(to_chips)
-        score(near_mid, turn // 2, turn * 3 // 4)
+        score(near_mid, 0, turn // 4, range(1, n_perm), 2 * unroll)
         relay_if(is_outer, 1)
-        score(near_mid, turn * 3 // 4, turn)
+        score(near_mid, turn // 4, turn // 2, range(1, n_perm), 2 * unroll)
         pl.when(is_mid)(lambda: passed(1))
         score(far_mid, 0, turn // 2)
         relay_if(is_mid, 0)
@@ -278,13 +291,15 @@
         score(far_mid, turn * 2 - 1, turn * 2, unroll=unroll // 2)
         pl.when(var_at != near_outer)(lambda: receive(block(near_outer), own_recv.at[0]))
         pl.when(is_outer)(lambda: passed(1))
+        found = widest()
         for slot in range(1, n_perm):
             slide(slot)
-            widen(slot)
+            widen(slot, found)
         hand_over()
         slide(0)
-        widen(0)
+        widen(0, found)
     else:
+        build_others()
         score(var_at)
         receive(block(var_of(0, 1 - core)), own_recv.at[0])
         score(var_of(0, 1 - core))
@@ -380,9 +395,10 @@
         packed = pl.pallas_call(
             functools.partial(kernel, (n_gene, n_var, n_perm)),
             out_shape=jax.ShapeDtypeStruct((width + 8, genes), jnp.float32),
-            in_specs=[vmem] * 4 + [smem],
+            in_specs=[pl.BlockSpec(memory_space=pl.ANY)] + [vmem] * 3 + [smem],
             out_specs=vmem,
             scratch_shapes=[
+                pltpu.VMEM((local, samples), jnp.bfloat16), dma,
                 pltpu.VMEM((n_var * local // PAD + 1, PAD, samples), jnp.bfloat16),
                 pltpu.VMEM((n_perm, groups, cols, samples), jnp.bfloat16),
                 pltpu.VMEM((genes, samples), jnp.bfloat16),

time: 65.7 us -> 63.9 us (0.973)
  Pallas kernels: 64.7 us -> 62.9 us
    pallas_call x1, Pallas kernels: 63.3 us -> 61.6 us  [shards(): pl.pallas_call(functools.partial(kernel, (n_gene, n_var, n_perm)), out_sh...]
where the time goes in v2:
time: 63.9 us; the launch traced here: 63.7 us
  Pallas kernels  62.9 us (98%)
  between operations  0.8 us (1%)
    pallas_call x1, Pallas kernels, shards(): pl.pallas_call(functools.partial(kernel, (n_gene, n_var, n_perm)), out_sh...  61.6 us
    pallas_call x1, Pallas kernels, shards(): pl.pallas_call(unpack, out_shape=(jax.ShapeDtypeStruct((width, genes), jn...  1.35 us

profile of v2, /device:TPU:0, one launch (start us, length us, event | category | flops | bytes accessed | tf_op | source)
XLA Modules:
  0.0 63.7 jit_solution(3333941397110775854)
XLA Ops:
  0.6 61.6 %shard_map.67.packed = f32[40,128]{1,0:T(8,128)} custom-call(bf16[768,768]{1,0:T(8,128)(2,1)} %bitcast.2, f32[128,768]{1,0:T(8,128)} %pheno.1, s32[32,768]{1,0:T(8,128)} %perms.1, s32[1,128]{1,0:T(1,128)} %bitcast.3, s32[128]{0:T(128)} %firsts.1), custom_call_target="tpu_custom_call" | custom-call | flops 43486543872 | bytes 1179648 | tf_op jit(solution)/shard_map/pallas_call | solution.py:395
  62.2 1.3 %shard_map.68 = (f32[32,128]{1,0:T(8,128)}, f32[2,128]{1,0:T(2,128)}, f32[2]{0:T(128)}) custom-call(f32[40,128]{1,0:T(8,128)} %shard_map.67.packed), custom_call_target="tpu_custom_call" | custom-call | tf_op jit(solution)/shard_map/pallas_call | solution.py:422
